TPU v7x, 128 devices: a whole 4x4x4 slice. The times are simulated.
128 devices in a mesh: row: 16 (over z, y_hi, core), col: 8 (over y_lo, x).
Axes of the slice: x: 4, y: 4 (y_hi: 2, y_lo: 2; y = y_hi * 2 + y_lo), z: 4, core: 2. Of those that a mesh axis runs over, the one named last changes fastest.
Arguments:
- left_prop: float32 [16, 8, 2, 512, 512], P('row', None, None, 'col'), may hold values from -0.1875 to 0.1875
- vertex: float32 [8, 2, 512, 512], P(None, None, ('row', 'col')), may hold values from -5 to 5
- right_prop: float32 [8, 16, 2, 512, 512], P(None, 'col', None, None, 'row'), may hold values from -0.1875 to 0.1875
- insertions: int32 [3], replicated, may hold values from 0 to 7
- window_start: int32 [2], replicated, may hold values from 0 to 255
Outputs:
- correlator: float32 [16, 16, 2, 512, 512], P('row', 'col')
Inputs may be any that keep to these rules, and one draw needn't show every extreme that they name: `insertions`: repeats may occur.
All inputs are finite; a program needn't handle non-finite values.
Results may differ from a plain program's by a relative error of at most 0.0001.
Values sent between devices are 32-bit elements; how exact they have to be, the bound alone decides.
No kernel may reach another device: no remote copies, remote signals or barrier semaphores. Data moves between devices by JAX's collectives and lax.ppermute only.
A program may use at most 128 MiB of HBM per device.

v0:
```python
import jax
import jax.numpy as jnp
from jax import lax
from jax.sharding import Mesh
from jax.sharding import PartitionSpec as P

NS = 8
LT = 256
ROW = ("row_0", "row_1", "row_2")
COL = ("col_0", "col_1")
ROW_COL = ("row_0", "row_1", "row_2", "col_0", "col_1")


def piece_ends(length, count):
    unit = 8 if length >= 8 * count else 1
    return [length // unit * k // count * unit for k in range(1, count)]


def all_blocks(x, axes, order):
    tiles = x[None]
    for k in order:
        tiles = lax.all_gather(tiles, axes[k], axis=0, tiled=True)
    held = [lax.axis_size(axes[k]) for k in reversed(order)]
    tiles = tiles.reshape(*held, *x.shape)
    turned = sorted(range(len(order)), key=lambda place: order[len(order) - 1 - place])
    return tiles.transpose(*turned, *range(len(order), tiles.ndim)).reshape(-1, *x.shape)


def in_order(tiles, dim):
    shape = list(tiles.shape[1:])
    shape[dim] *= tiles.shape[0]
    return jnp.moveaxis(tiles, 0, dim).reshape(shape)


def spread_gather(x, axes, dim):
    cut = max(range(max(1, x.ndim - 1)), key=lambda d: x.shape[d])
    count, finished = (len(axes), [])
    for leading, share in enumerate(jnp.split(x, piece_ends(x.shape[cut], count), axis=cut)):
        if share.size:
            order = [(leading - k) % count for k in range(count)]
            finished.append(all_blocks(share, axes, order))
    return in_order(jnp.concatenate(finished, axis=cut + 1), dim)


def complex_product(first, second):
    highest = lax.Precision.HIGHEST
    first_re, first_im = (first[..., 0, :, :], first[..., 1, :, :])
    second_re, second_im = (second[..., 0, :, :], second[..., 1, :, :])
    real_part = jnp.matmul(first_re, second_re, precision=highest) - jnp.matmul(
        first_im, second_im, precision=highest
    )
    imag_part = jnp.matmul(first_re, second_im, precision=highest) + jnp.matmul(
        first_im, second_re, precision=highest
    )
    return jnp.stack([real_part, imag_part], axis=-3)


def contract_with(left_operand, column_piece):
    summed = complex_product(left_operand[:, 0, None], column_piece[0][None])
    for which in range(1, column_piece.shape[0]):
        summed = summed + complex_product(left_operand[:, which, None], column_piece[which][None])
    return summed


def per_device(left_prop, vertex, right_prop, insertions, window_start):
    source_count = left_prop.shape[0]
    sink_count = right_prop.shape[1]
    source_slots = lax.axis_index(ROW) * source_count + jnp.arange(source_count, dtype=jnp.int32)
    sink_slots = lax.axis_index(COL) * sink_count + jnp.arange(sink_count, dtype=jnp.int32)
    slice_times = insertions * (LT // NS)
    source_times = (window_start[0] + source_slots) % LT
    sink_times = (window_start[1] + sink_slots) % LT
    left_sign = jnp.where(slice_times[None, :] < source_times[:, None], -1.0, 1.0).astype(
        jnp.float32
    )
    right_sign = jnp.where(sink_times[None, :] < slice_times[:, None], -1.0, 1.0).astype(
        jnp.float32
    )
    chosen_left = jnp.take(left_prop, insertions, axis=1) * left_sign[:, :, None, None, None]
    chosen_right = jnp.take(right_prop, insertions, axis=0) * right_sign[:, :, None, None, None]
    vertex_part = jnp.take(vertex, insertions, axis=0)
    vertex_full = spread_gather(vertex_part, ROW_COL, 2)
    left_full = lax.all_gather(chosen_left, COL, axis=3, tiled=True)
    vertex_right = complex_product(vertex_full[:, None], chosen_right)
    result = contract_with(left_full, lax.all_gather(vertex_right, ROW, axis=4, tiled=True))
    return result


def solution(mesh):
    finer = Mesh(mesh.devices.reshape(4, 2, 2, 2, 4), ("row_0", "row_1", "row_2", "col_0", "col_1"))
    return jax.shard_map(
        per_device,
        mesh=finer,
        in_specs=(
            P(ROW, None, None, COL, None),
            P(None, None, ROW_COL, None),
            P(None, COL, None, None, ROW),
            P(),
            P(),
        ),
        out_specs=P(ROW, COL, None, None, None),
        check_vma=False,
    )
```

profile of v0, /device:TPU:1, one launch (start us, length us, event | category | flops | bytes accessed | tf_op | source)
XLA Modules:
  0.0 401.7 jit_solution(11193293117327762396)
XLA Ops:
  6.5 0.8 compare_and_fusion
  7.4 0.7 broadcast_multiply_fusion
  8.0 1.5 gather_fusion.1
  9.5 0.1 broadcast_select_fusion
  9.6 5.5 %all-gather = f32[6,2,1,512]{3,1,2,0:T(2,128)S(1)} all-gather(f32[3,2,1,512]{3,1,2,0:T(2,128)S(1)} %copy.62), channel_id=2, replica_groups=mesh['row_0'=4,'row_1'=2,'row_2'=2,'col_0'=2,'col_1'=4] {'row_1'}, dimensions={0}, use_global_device_ids=true | all-gather | bytes 36864 | tf_op jit(solution)/shard_map/all_gather | solution.py:22
  15.1 10.3 %all_gather.68 = f32[8,3,2,1,512]{4,2,3,1,0:T(2,128)S(1)} all-gather(f32[2,3,2,1,512]{4,2,3,1,0:T(2,128)S(1)} %bitcast.186), channel_id=1, replica_groups=mesh['row_0'=4,'row_1'=2,'row_2'=2,'col_0'=2,'col_1'=4] {'row_0'}, dimensions={0}, use_global_device_ids=true | all-gather | bytes 122880 | tf_op jit(solution)/shard_map/all_gather | solution.py:22
  25.4 10.4 %all_gather.69 = f32[32,3,2,1,512]{4,2,3,1,0:T(2,128)S(1)} all-gather(f32[8,3,2,1,512]{4,2,3,1,0:T(2,128)S(1)} %all_gather.68), channel_id=1, replica_groups=mesh['row_0'=4,'row_1'=2,'row_2'=2,'col_0'=2,'col_1'=4] {'col_1'}, dimensions={0}, use_global_device_ids=true | all-gather | bytes 491520 | tf_op jit(solution)/shard_map/all_gather | solution.py:22
  35.9 7.4 %all_gather.70 = f32[64,3,2,1,512]{4,2,3,1,0:T(2,128)} all-gather(f32[32,3,2,1,512]{4,2,3,1,0:T(2,128)S(1)} %all_gather.69), channel_id=1, replica_groups=mesh['row_0'=4,'row_1'=2,'row_2'=2,'col_0'=2,'col_1'=4] {'col_0'}, dimensions={0}, use_global_device_ids=true | all-gather | bytes 1179648 | tf_op jit(solution)/shard_map/all_gather | solution.py:22
  43.3 0.0 all-gather.15.cloned.1.call-start
  43.4 9.9 %all-gather.1 = f32[6,2,1,512]{3,1,2,0:T(2,128)S(1)} all-gather(f32[3,2,1,512]{3,1,2,0:T(2,128)S(1)} %copy.65), channel_id=3, replica_groups=mesh['row_0'=4,'row_1'=2,'row_2'=2,'col_0'=2,'col_1'=4] {'row_2'}, dimensions={0}, use_global_device_ids=true | all-gather | bytes 36864 | tf_op jit(solution)/shard_map/all_gather | solution.py:22
  53.3 4.8 %all_gather.73 = f32[4,3,2,1,512]{4,2,3,1,0:T(2,128)S(1)} all-gather(f32[2,3,2,1,512]{4,2,3,1,0:T(2,128)S(1)} %bitcast.184), channel_id=1, replica_groups=mesh['row_0'=4,'row_1'=2,'row_2'=2,'col_0'=2,'col_1'=4] {'row_1'}, dimensions={0}, use_global_device_ids=true | all-gather | bytes 73728 | tf_op jit(solution)/shard_map/all_gather | solution.py:22
  58.1 9.2 %all_gather.74 = f32[16,3,2,1,512]{4,2,3,1,0:T(2,128)S(1)} all-gather(f32[4,3,2,1,512]{4,2,3,1,0:T(2,128)S(1)} %all_gather.73), channel_id=1, replica_groups=mesh['row_0'=4,'row_1'=2,'row_2'=2,'col_0'=2,'col_1'=4] {'row_0'}, dimensions={0}, use_global_device_ids=true | all-gather | bytes 245760 | tf_op jit(solution)/shard_map/all_gather | solution.py:22
  67.4 11.5 %all_gather.75 = f32[64,3,2,1,512]{4,2,3,1,0:T(2,128)} all-gather(f32[16,3,2,1,512]{4,2,3,1,0:T(2,128)S(1)} %all_gather.74), channel_id=1, replica_groups=mesh['row_0'=4,'row_1'=2,'row_2'=2,'col_0'=2,'col_1'=4] {'col_1'}, dimensions={0}, use_global_device_ids=true | all-gather | bytes 983040 | tf_op jit(solution)/shard_map/all_gather | solution.py:22
  78.8 0.0 all-gather.17.cloned.1.call-start
  78.9 3.6 all-gather.2
  82.5 9.5 %all_gather.78 = f32[4,3,2,1,512]{4,2,3,1,0:T(2,128)S(1)} all-gather(f32[2,3,2,1,512]{4,2,3,1,0:T(2,128)S(1)} %bitcast.185), channel_id=1, replica_groups=mesh['row_0'=4,'row_1'=2,'row_2'=2,'col_0'=2,'col_1'=4] {'row_2'}, dimensions={0}, use_global_device_ids=true | all-gather | bytes 73728 | tf_op jit(solution)/shard_map/all_gather | solution.py:22
  92.1 5.1 %all_gather.79 = f32[8,3,2,1,512]{4,2,3,1,0:T(2,128)S(1)} all-gather(f32[4,3,2,1,512]{4,2,3,1,0:T(2,128)S(1)} %all_gather.78), channel_id=1, replica_groups=mesh['row_0'=4,'row_1'=2,'row_2'=2,'col_0'=2,'col_1'=4] {'row_1'}, dimensions={0}, use_global_device_ids=true | all-gather | bytes 147456 | tf_op jit(solution)/shard_map/all_gather | solution.py:22
  97.2 10.7 %all_gather.80 = f32[32,3,2,1,512]{4,2,3,1,0:T(2,128)} all-gather(f32[8,3,2,1,512]{4,2,3,1,0:T(2,128)S(1)} %all_gather.79), channel_id=1, replica_groups=mesh['row_0'=4,'row_1'=2,'row_2'=2,'col_0'=2,'col_1'=4] {'row_0'}, dimensions={0}, use_global_device_ids=true | all-gather | bytes 491520 | tf_op jit(solution)/shard_map/all_gather | solution.py:22
  107.9 0.0 all-gather.19.cloned.1.call-start
  108.0 9.1 %all-gather.3 = f32[12,2,1,512]{3,1,2,0:T(2,128)S(1)} all-gather(f32[3,2,1,512]{3,1,2,0:T(2,128)S(1)} %copy.71), channel_id=5, replica_groups=mesh['row_0'=4,'row_1'=2,'row_2'=2,'col_0'=2,'col_1'=4] {'col_1'}, dimensions={0}, use_global_device_ids=true | all-gather | bytes 61440 | tf_op jit(solution)/shard_map/all_gather | solution.py:22
  117.1 0.1 copy.72
  117.2 3.9 all_gather.83
  121.1 9.2 %all_gather.84 = f32[16,3,2,1,512]{4,3,0,1,2:T(1,128)S(1)} all-gather(f32[8,3,2,1,512]{4,3,0,1,2:T(1,128)S(1)} %all_gather.83), channel_id=1, replica_groups=mesh['row_0'=4,'row_1'=2,'row_2'=2,'col_0'=2,'col_1'=4] {'row_2'}, dimensions={0}, use_global_device_ids=true | all-gather | bytes 294912 | tf_op jit(solution)/shard_map/all_gather | solution.py:22
  130.3 9.6 %all_gather.85 = f32[32,3,2,1,512]{4,3,0,1,2:T(1,128)} all-gather(f32[16,3,2,1,512]{4,3,0,1,2:T(1,128)S(1)} %all_gather.84), channel_id=1, replica_groups=mesh['row_0'=4,'row_1'=2,'row_2'=2,'col_0'=2,'col_1'=4] {'row_1'}, dimensions={0}, use_global_device_ids=true | all-gather | bytes 589824 | tf_op jit(solution)/shard_map/all_gather | solution.py:22
  139.9 0.0 all-gather.11.cloned.1.call-start
  140.0 0.5 fusion.22
  141.2 0.6 gather_fusion
  141.9 1.1 fusion.17
  143.0 2.2 gather_fusion.2
  145.2 0.6 and_select_fusion
  145.8 0.1 compare_select_fusion.3
  145.8 0.2 fusion.18
  146.0 0.1 fusion.20
  146.1 3.6 copy.64
  149.7 3.7 reshape.208
  153.4 3.6 copy.67
  157.0 4.3 %reshape.210 = f32[128,3,2,1,512]{4,3,0,1,2:T(1,128)} reshape(f32[4,2,2,2,4,3,2,1,512]{8,4,3,2,1,0,5,6,7:T(4,128)} %copy.67) | data formatting | bytes 3145728 | tf_op jit(solution)/shard_map/reshape | solution.py:26
  161.3 3.6 copy.70
  164.9 4.2 %reshape.212 = f32[128,3,2,1,512]{4,3,0,1,2:T(1,128)} reshape(f32[4,2,2,2,4,3,2,1,512]{8,4,3,2,1,0,5,6,7:T(4,128)} %copy.70) | data formatting | bytes 3145728 | tf_op jit(solution)/shard_map/reshape | solution.py:26
  169.1 3.9 all-gather.19.cloned.1.call-done
  173.0 8.6 %maximum_bitcast_fusion = f32[3,2,128,4,512]{4,3,2,0,1:T(4,128)} fusion(f32[128,3,2,1,512]{4,3,0,1,2:T(1,128)} %all-gather.19.cloned.1.call-done, f32[128,3,2,1,512]{4,3,0,1,2:T(1,128)} %reshape.212, f32[128,3,2,1,512]{4,3,0,1,2:T(1,128)} %reshape.210, f32[128,3,2,1,512]{4,3,0,1,2:T(1,128)S(1)} %reshape.208), kind=kLoop, calls=%fused_computation.3 | loop fusion | flops 4718592 | bytes 12582912 | tf_op jit(solution)/shard_map/transpose | solution.py:32
  181.6 8.2 %broadcast_in_dim_reshape.3 = f32[3,1,2,512,512]{4,3,0,2,1:T(8,128)} reshape(f32[3,2,128,4,512]{4,3,2,0,1:T(4,128)} %maximum_bitcast_fusion) | data formatting | bytes 12582912 | tf_op jit(solution)/shard_map/broadcast_in_dim;reshape | solution.py:84
  189.8 5.2 %fusion.1 = f32[3,512,64]{1,2,0:S(1)} fusion(f32[3,512,64]{1,2,0:T(8,128)S(1)} %bitcast.174, f32[3,1,2,512,512]{4,3,0,2,1:T(8,128)} %broadcast_in_dim_reshape.3), kind=kOutput, calls=%fused_computation.8 | convolution fusion | flops 603979776 | bytes 3932160
  195.1 5.1 %fusion.4 = f32[3,512,64]{1,2,0:S(1)} fusion(f32[3,512,64]{1,2,0:T(8,128)S(1)} %bitcast.175, f32[3,1,2,512,512]{4,3,0,2,1:T(8,128)} %broadcast_in_dim_reshape.3), kind=kOutput, calls=%fused_computation.11 | convolution fusion | flops 603979776 | bytes 3932160
  200.1 3.2 fusion.3
  203.3 3.2 fusion.2
  206.5 0.1 add_bitcast_fusion.3
  206.6 0.9 pad_maximum_fusion
  207.6 38.9 %all-gather.11.cloned.1.call-done = f32[1,3,2,512,512]{4,3,2,1,0:T(8,128)} async-done(((f32[1,3,2,64,512]{4,3,2,1,0:T(8,128)}), f32[1,3,2,512,512]{4,3,2,1,0:T(8,128)}) %all-gather.11.cloned.1.call-update) | async-done | bytes 6291472 | tf_op jit(solution)/shard_map/all_gather | solution.py:83
  246.5 92.3 %all-gather.21.cloned.1.call-done = f32[3,2,2,512,512]{3,4,1,0,2:T(8,128)} async-done(((f32[3,2,2,512,32]{3,4,1,0,2:T(8,128)}), f32[3,2,2,512,512]{3,4,1,0,2:T(8,128)}) %all-gather.21.cloned.1.call-update) | async-done | bytes 12582928 | tf_op jit(solution)/shard_map/all_gather | solution.py:85
  338.9 5.8 %fusion.13 = f32[512,2,512]{2,0,1:T(8,128)S(1)} fusion(f32[3,2,2,512,512]{3,4,1,0,2:T(8,128)} %all-gather.21.cloned.1.call-done, f32[1,3,2,512,512]{4,3,2,1,0:T(8,128)} %all-gather.11.cloned.1.call-done), kind=kOutput, calls=%fused_computation.32 | convolution fusion | flops 3221225472 | bytes 5242880 | tf_op jit(solution)/shard_map/dot_general | solution.py:52
  344.7 5.5 %fusion.9 = f32[512,2,512]{2,0,1:T(8,128)S(1)} fusion(f32[3,2,2,512,512]{3,4,1,0,2:T(8,128)} %all-gather.21.cloned.1.call-done, f32[1,3,2,512,512]{4,3,2,1,0:T(8,128)} %all-gather.11.cloned.1.call-done), kind=kOutput, calls=%fused_computation.28 | convolution fusion | flops 3221225472 | bytes 5242880 | tf_op jit(solution)/shard_map/dot_general | solution.py:52
  350.2 5.6 %fusion.5 = f32[512,2,512]{2,0,1:T(8,128)S(1)} fusion(f32[3,2,2,512,512]{3,4,1,0,2:T(8,128)} %all-gather.21.cloned.1.call-done, f32[1,3,2,512,512]{4,3,2,1,0:T(8,128)} %all-gather.11.cloned.1.call-done), kind=kOutput, calls=%fused_computation.24 | convolution fusion | flops 3221225472 | bytes 5242880 | tf_op jit(solution)/shard_map/dot_general | solution.py:52
  355.9 5.1 %fusion.14 = f32[512,2,512]{2,0,1:T(8,128)S(1)} fusion(f32[3,2,2,512,512]{3,4,1,0,2:T(8,128)S(1)} %copy-done.3, f32[1,3,2,512,512]{4,3,2,1,0:T(8,128)} %all-gather.11.cloned.1.call-done), kind=kOutput, calls=%fused_computation.33 | convolution fusion | flops 3221225472 | bytes 5242880 | tf_op jit(solution)/shard_map/dot_general | solution.py:49
  361.0 3.6 fusion.10
  364.6 3.6 fusion.6
  368.1 3.6 add_bitcast_fusion
  371.7 4.0 %add_bitcast_fusion.1 = f32[1,2,1,512,512]{4,3,1,2,0:T(8,128)S(1)} fusion(f32[512,2,512]{2,0,1:T(8,128)S(1)} %fusion.9, f32[3,2,2,512,512]{3,4,1,0,2:T(8,128)S(1)} %copy-done.3, f32[1,3,2,512,512]{4,3,2,1,0:T(8,128)S(1)} %copy-done.4), kind=kOutput, calls=%fused_computation.20 | convolution fusion | flops 3221749760 | bytes 7340032 | tf_op jit(solution)/shard_map/dot_general | solution.py:52
  375.8 3.6 add_bitcast_fusion.2
  379.4 3.6 subtract_bitcast_fusion
  383.0 3.8 subtract_bitcast_fusion.1
  386.8 3.7 subtract_bitcast_fusion.2
  390.6 1.6 fusion
  392.2 2.5 copy.86
  (32 shorter events, 0.3 us)
Async XLA Ops:
  6.5 134.7 %copy-start = (f32[1,8,2,64,512]{4,3,2,1,0:T(8,128)S(1)}, f32[1,8,2,64,512]{4,3,2,1,0:T(8,128)}, u32[]{:S(2)}) copy-start(f32[1,8,2,64,512]{4,3,2,1,0:T(8,128)} %param.5) | copy-start | bytes 6291460
  6.5 139.6 %all-gather.13.cloned.1.call-start = ((), (), s32[]{:S(2)}) async-start(), calls=%async_computation.1 | async-start | bytes 2359296 | tf_op jit(solution)/shard_map/all_gather | solution.py:22
  43.3 96.7 %copy-start.5 = (s32[2]{0:T(128)S(1)}, s32[2]{0:T(128)}, u32[]{:S(2)}) copy-start(s32[2]{0:T(128)} %param.9) | copy-start | bytes 28
  43.3 110.1 %all-gather.15.cloned.1.call-start = ((), (), s32[]{:S(2)}) async-start(), calls=%async_computation.2 | async-start | bytes 2359296 | tf_op jit(solution)/shard_map/all_gather | solution.py:22
  67.4 74.5 %copy-start.6 = (s32[3]{0:T(128)S(1)}, s32[3]{0:T(128)}, u32[]{:S(2)}) copy-start(s32[3]{0:T(128)} %param.8) | copy-start | bytes 40
  78.8 82.4 %all-gather.17.cloned.1.call-start = ((), (), s32[]{:S(2)}) async-start(), calls=%async_computation.3 | async-start | bytes 1966080 | tf_op jit(solution)/shard_map/all_gather | solution.py:22
  107.9 65.1 %all-gather.19.cloned.1.call-start = ((), (), s32[]{:S(2)}) async-start(), calls=%async_computation.4 | async-start | bytes 1966080 | tf_op jit(solution)/shard_map/all_gather | solution.py:22
  139.9 106.6 %all-gather.11.cloned.1.call-start = ((), (), s32[]{:S(2)}) async-start(), calls=%async_computation | async-start | bytes 7077888 | tf_op jit(solution)/shard_map/all_gather | solution.py:83
  142.9 195.9 %all-gather.21.cloned.1.call-start = ((), (), s32[]{:S(2)}) async-start(), calls=%async_computation.5 | async-start | bytes 13369344 | tf_op jit(solution)/shard_map/all_gather | solution.py:85
  189.8 10.3 %copy-start.2 = (f32[3,1,2,512,512]{4,3,0,2,1:T(8,128)S(1)}, f32[3,1,2,512,512]{4,3,0,2,1:T(8,128)}, u32[]{:S(2)}) copy-start(f32[3,1,2,512,512]{4,3,0,2,1:T(8,128)} %broadcast_in_dim_reshape.3) | copy-start | bytes 18874372
  338.9 17.0 %copy-start.3 = (f32[3,2,2,512,512]{3,4,1,0,2:T(8,128)S(1)}, f32[3,2,2,512,512]{3,4,1,0,2:T(8,128)}, u32[]{:S(2)}) copy-start(f32[3,2,2,512,512]{3,4,1,0,2:T(8,128)} %all-gather.21.cloned.1.call-done) | copy-start | bytes 37748740
  350.2 10.7 %copy-start.4 = (f32[1,3,2,512,512]{4,3,2,1,0:T(8,128)S(1)}, f32[1,3,2,512,512]{4,3,2,1,0:T(8,128)}, u32[]{:S(2)}) copy-start(f32[1,3,2,512,512]{4,3,2,1,0:T(8,128)} %all-gather.11.cloned.1.call-done) | copy-start | bytes 18874372
  390.6 4.1 %copy-start.1 = (f32[1,8,2,64,512]{4,3,2,1,0:T(8,128)S(1)}, f32[1,8,2,64,512]{4,3,2,1,0:T(8,128)}, u32[]{:S(2)}) copy-start(f32[1,8,2,64,512]{4,3,2,1,0:T(8,128)} %param.5) | copy-start | bytes 6291460
Sparse Core Ops, SparseCore 0:
  43.4 21.2 all-gather.12
  79.0 36.6 all-gather.14
  117.4 27.3 all-gather.16
  146.3 26.6 all-gather.18
  174.5 71.9 all-gather.10
  248.8 89.9 all-gather.20
where the time goes:
time: 406 us; the launch traced here: 402 us
  waiting for transfers between devices  135 us (33%)
  blocking collectives  130 us (32%)
  matrix products  68.2 us (17%)
  local copies, waits for them, and re-layouts  38.6 us (10%)
  other arithmetic  14.7 us (4%)
  between operations  14.7 us (4%)
    all_gather x16, blocking collectives, all_blocks(): tiles = lax.all_gather(tiles, axes[k], axis=0, tiled=True)  130 us
    all_gather x1, waiting for transfers between devices, per_device(): lax.all_gather(vertex_right, ROW, axis=4, tiled=True)  92.3 us
    all_gather x1, waiting for transfers between devices, per_device(): left_full = lax.all_gather(chosen_left, COL, axis=3, tiled=True)  38.9 us
    dot_general x3, matrix products, complex_product(): jnp.matmul(first_im, second_re, precision=highest)  17 us
    unnamed x4, matrix products  16.6 us
    reshape x3, local copies, waits for them, and re-layouts, all_blocks(): tiles.transpose(*turned, *range(len(order), tiles.ndim))  12.2 us
    dot_general x3, matrix products, complex_product(): jnp.matmul(first_re, second_re, precision=highest)  12.2 us
    dot_general x3, matrix products, complex_product(): jnp.matmul(first_re, second_im, precision=highest)  11.3 us
  transfers between devices with their start and end apart: 6, of which 3 were waited for; matrix products, arithmetic and copies ran while one was open for 16% of the time, Pallas kernels for 0%

commit v1 on v0

--- a/solution.py
+++ b/solution.py
@@ -82,7 +82,7 @@
     vertex_full = spread_gather(vertex_part, ROW_COL, 2)
     left_full = lax.all_gather(chosen_left, COL, axis=3, tiled=True)
     vertex_right = complex_product(vertex_full[:, None], chosen_right)
-    result = contract_with(left_full, lax.all_gather(vertex_right, ROW, axis=4, tiled=True))
+    result = contract_with(left_full, jnp.concatenate(lax.all_gather(vertex_right, ROW), axis=4))
     return result
 
 

time: 406 us -> 433 us (1.067)
  local copies, waits for them, and re-layouts: 38.6 us -> 62 us
  waiting for transfers between devices: 135 us -> 142 us
    all_gather x0 -> x1, local copies, waits for them, and re-layouts: none -> 12 us  [per_device(): lax.all_gather(vertex_right, ROW)]
    slice x0 -> x1, local copies, waits for them, and re-layouts: none -> 10.6 us  [contract_with(): column_piece[which][None]]
    all_gather x1, waiting for transfers between devices: 38.9 us -> 48.1 us  [per_device(): left_full = lax.all_gather(chosen_left, COL, axis=3, tiled=True)]
    dot_general x3, matrix products: 17 us -> 12.3 us  [complex_product(): jnp.matmul(first_im, second_re, precision=highest)]
  transfers between devices with their start and end apart: 6 -> 6, of which waited for: 3 -> 3; matrix products, arithmetic and copies ran while one was open for 16% -> 12% of each run, Pallas kernels for 0% -> 0%
where the time goes in v1:
time: 433 us; the launch traced here: 429 us
  waiting for transfers between devices  142 us (33%)
  blocking collectives  130 us (30%)
  matrix products  65.4 us (15%)
  local copies, waits for them, and re-layouts  62 us (14%)
  other arithmetic  15.1 us (3%)
  between operations  14.7 us (3%)
    all_gather x16, blocking collectives, all_blocks(): tiles = lax.all_gather(tiles, axes[k], axis=0, tiled=True)  130 us
    all_gather x1, waiting for transfers between devices, per_device(): lax.all_gather(vertex_right, ROW)  88.6 us
    all_gather x1, waiting for transfers between devices, per_device(): left_full = lax.all_gather(chosen_left, COL, axis=3, tiled=True)  48.1 us
    unnamed x4, matrix products  16.6 us
    dot_general x3, matrix products, complex_product(): jnp.matmul(first_re, second_re, precision=highest)  14.5 us
    reshape x3, local copies, waits for them, and re-layouts, all_blocks(): tiles.transpose(*turned, *range(len(order), tiles.ndim))  13.3 us
    dot_general x3, matrix products, complex_product(): jnp.matmul(first_im, second_re, precision=highest)  12.3 us
    all_gather x1, local copies, waits for them, and re-layouts, per_device(): lax.all_gather(vertex_right, ROW)  12 us
  transfers between devices with their start and end apart: 6, of which 3 were waited for; matrix products, arithmetic and copies ran while one was open for 12% of the time, Pallas kernels for 0%

profile of v1, /device:TPU:1, one launch (start us, length us, event | category | flops | bytes accessed | tf_op | source)
XLA Modules:
  0.0 429.4 jit_solution(12857592787774247642)
XLA Ops:
  6.5 0.8 broadcast_multiply_fusion
  7.3 0.7 compare_and_fusion
  8.0 1.5 gather_fusion.1
  9.5 0.1 broadcast_select_fusion
  9.6 5.5 %all-gather = f32[6,2,1,512]{3,1,2,0:T(2,128)S(1)} all-gather(f32[3,2,1,512]{3,1,2,0:T(2,128)S(1)} %copy.43), channel_id=2, replica_groups=mesh['row_0'=4,'row_1'=2,'row_2'=2,'col_0'=2,'col_1'=4] {'row_1'}, dimensions={0}, use_global_device_ids=true | all-gather | bytes 36864 | tf_op jit(solution)/shard_map/all_gather | solution.py:22
  15.1 10.3 %all_gather.71 = f32[8,3,2,1,512]{4,2,3,1,0:T(2,128)S(1)} all-gather(f32[2,3,2,1,512]{4,2,3,1,0:T(2,128)S(1)} %bitcast.219), channel_id=1, replica_groups=mesh['row_0'=4,'row_1'=2,'row_2'=2,'col_0'=2,'col_1'=4] {'row_0'}, dimensions={0}, use_global_device_ids=true | all-gather | bytes 122880 | tf_op jit(solution)/shard_map/all_gather | solution.py:22
  25.4 10.4 %all_gather.72 = f32[32,3,2,1,512]{4,2,3,1,0:T(2,128)S(1)} all-gather(f32[8,3,2,1,512]{4,2,3,1,0:T(2,128)S(1)} %all_gather.71), channel_id=1, replica_groups=mesh['row_0'=4,'row_1'=2,'row_2'=2,'col_0'=2,'col_1'=4] {'col_1'}, dimensions={0}, use_global_device_ids=true | all-gather | bytes 491520 | tf_op jit(solution)/shard_map/all_gather | solution.py:22
  35.9 7.4 %all_gather.73 = f32[64,3,2,1,512]{4,2,3,1,0:T(2,128)} all-gather(f32[32,3,2,1,512]{4,2,3,1,0:T(2,128)S(1)} %all_gather.72), channel_id=1, replica_groups=mesh['row_0'=4,'row_1'=2,'row_2'=2,'col_0'=2,'col_1'=4] {'col_0'}, dimensions={0}, use_global_device_ids=true | all-gather | bytes 1179648 | tf_op jit(solution)/shard_map/all_gather | solution.py:22
  43.4 9.9 %all-gather.1 = f32[6,2,1,512]{3,1,2,0:T(2,128)S(1)} all-gather(f32[3,2,1,512]{3,1,2,0:T(2,128)S(1)} %copy.46), channel_id=3, replica_groups=mesh['row_0'=4,'row_1'=2,'row_2'=2,'col_0'=2,'col_1'=4] {'row_2'}, dimensions={0}, use_global_device_ids=true | all-gather | bytes 36864 | tf_op jit(solution)/shard_map/all_gather | solution.py:22
  53.3 4.8 %all_gather.76 = f32[4,3,2,1,512]{4,2,3,1,0:T(2,128)S(1)} all-gather(f32[2,3,2,1,512]{4,2,3,1,0:T(2,128)S(1)} %bitcast.217), channel_id=1, replica_groups=mesh['row_0'=4,'row_1'=2,'row_2'=2,'col_0'=2,'col_1'=4] {'row_1'}, dimensions={0}, use_global_device_ids=true | all-gather | bytes 73728 | tf_op jit(solution)/shard_map/all_gather | solution.py:22
  58.1 9.2 %all_gather.77 = f32[16,3,2,1,512]{4,2,3,1,0:T(2,128)S(1)} all-gather(f32[4,3,2,1,512]{4,2,3,1,0:T(2,128)S(1)} %all_gather.76), channel_id=1, replica_groups=mesh['row_0'=4,'row_1'=2,'row_2'=2,'col_0'=2,'col_1'=4] {'row_0'}, dimensions={0}, use_global_device_ids=true | all-gather | bytes 245760 | tf_op jit(solution)/shard_map/all_gather | solution.py:22
  67.4 11.3 %all_gather.78 = f32[64,3,2,1,512]{4,2,3,1,0:T(2,128)} all-gather(f32[16,3,2,1,512]{4,2,3,1,0:T(2,128)S(1)} %all_gather.77), channel_id=1, replica_groups=mesh['row_0'=4,'row_1'=2,'row_2'=2,'col_0'=2,'col_1'=4] {'col_1'}, dimensions={0}, use_global_device_ids=true | all-gather | bytes 983040 | tf_op jit(solution)/shard_map/all_gather | solution.py:22
  78.8 3.6 all-gather.2
  82.4 9.5 %all_gather.81 = f32[4,3,2,1,512]{4,2,3,1,0:T(2,128)S(1)} all-gather(f32[2,3,2,1,512]{4,2,3,1,0:T(2,128)S(1)} %bitcast.218), channel_id=1, replica_groups=mesh['row_0'=4,'row_1'=2,'row_2'=2,'col_0'=2,'col_1'=4] {'row_2'}, dimensions={0}, use_global_device_ids=true | all-gather | bytes 73728 | tf_op jit(solution)/shard_map/all_gather | solution.py:22
  91.9 5.1 %all_gather.82 = f32[8,3,2,1,512]{4,2,3,1,0:T(2,128)S(1)} all-gather(f32[4,3,2,1,512]{4,2,3,1,0:T(2,128)S(1)} %all_gather.81), channel_id=1, replica_groups=mesh['row_0'=4,'row_1'=2,'row_2'=2,'col_0'=2,'col_1'=4] {'row_1'}, dimensions={0}, use_global_device_ids=true | all-gather | bytes 147456 | tf_op jit(solution)/shard_map/all_gather | solution.py:22
  97.0 10.7 %all_gather.83 = f32[32,3,2,1,512]{4,2,3,1,0:T(2,128)} all-gather(f32[8,3,2,1,512]{4,2,3,1,0:T(2,128)S(1)} %all_gather.82), channel_id=1, replica_groups=mesh['row_0'=4,'row_1'=2,'row_2'=2,'col_0'=2,'col_1'=4] {'row_0'}, dimensions={0}, use_global_device_ids=true | all-gather | bytes 491520 | tf_op jit(solution)/shard_map/all_gather | solution.py:22
  107.8 0.0 all-gather.20.cloned.1.call-start
  107.9 9.1 %all-gather.3 = f32[12,2,1,512]{3,1,2,0:T(2,128)S(1)} all-gather(f32[3,2,1,512]{3,1,2,0:T(2,128)S(1)} %copy.52), channel_id=5, replica_groups=mesh['row_0'=4,'row_1'=2,'row_2'=2,'col_0'=2,'col_1'=4] {'col_1'}, dimensions={0}, use_global_device_ids=true | all-gather | bytes 61440 | tf_op jit(solution)/shard_map/all_gather | solution.py:22
  117.0 0.1 copy.53
  117.0 3.9 all_gather.86
  120.9 9.2 %all_gather.87 = f32[16,3,2,1,512]{4,3,0,1,2:T(1,128)S(1)} all-gather(f32[8,3,2,1,512]{4,3,0,1,2:T(1,128)S(1)} %all_gather.86), channel_id=1, replica_groups=mesh['row_0'=4,'row_1'=2,'row_2'=2,'col_0'=2,'col_1'=4] {'row_2'}, dimensions={0}, use_global_device_ids=true | all-gather | bytes 294912 | tf_op jit(solution)/shard_map/all_gather | solution.py:22
  130.2 9.6 %all_gather.88 = f32[32,3,2,1,512]{4,3,0,1,2:T(1,128)} all-gather(f32[16,3,2,1,512]{4,3,0,1,2:T(1,128)S(1)} %all_gather.87), channel_id=1, replica_groups=mesh['row_0'=4,'row_1'=2,'row_2'=2,'col_0'=2,'col_1'=4] {'row_1'}, dimensions={0}, use_global_device_ids=true | all-gather | bytes 589824 | tf_op jit(solution)/shard_map/all_gather | solution.py:22
  139.9 2.2 gather_fusion.2
  142.1 0.6 fusion.23
  142.7 0.7 and_select_fusion
  143.3 0.1 compare_select_fusion.3
  143.4 0.2 fusion.18
  143.6 0.1 fusion.21
  143.7 3.6 copy.45
  147.3 4.7 %reshape.215 = f32[128,3,2,1,512]{4,3,0,1,2:T(1,128)} reshape(f32[4,2,2,2,4,3,2,1,512]{8,4,3,2,1,0,5,6,7:T(4,128)} %copy.45) | data formatting | bytes 3145728 | tf_op jit(solution)/shard_map/reshape | solution.py:26
  152.0 3.6 copy.48
  155.5 4.3 %reshape.217 = f32[128,3,2,1,512]{4,3,0,1,2:T(1,128)} reshape(f32[4,2,2,2,4,3,2,1,512]{8,4,3,2,1,0,5,6,7:T(4,128)} %copy.48) | data formatting | bytes 3145728 | tf_op jit(solution)/shard_map/reshape | solution.py:26
  159.8 3.6 copy.51
  163.4 4.3 reshape.219
  167.7 5.2 %all-gather.20.cloned.1.call-done = f32[128,3,2,1,512]{4,3,0,1,2:T(1,128)} async-done(((f32[32,3,2,1,512]{4,3,0,1,2:T(1,128)}), f32[128,3,2,1,512]{4,3,0,1,2:T(1,128)}) %all-gather.20.cloned.1.call-update) | async-done | bytes 1572880 | tf_op jit(solution)/shard_map/all_gather | solution.py:22
  172.9 8.9 %maximum_bitcast_fusion = f32[3,2,128,4,512]{4,3,2,0,1:T(4,128)} fusion(f32[128,3,2,1,512]{4,3,0,1,2:T(1,128)} %all-gather.20.cloned.1.call-done, f32[128,3,2,1,512]{4,3,0,1,2:T(1,128)} %reshape.219, f32[128,3,2,1,512]{4,3,0,1,2:T(1,128)} %reshape.217, f32[128,3,2,1,512]{4,3,0,1,2:T(1,128)} %reshape.215), kind=kLoop, calls=%fused_computation.4 | loop fusion | flops 4718592 | bytes 12582912 | tf_op jit(solution)/shard_map/transpose | solution.py:32
  181.8 7.8 %broadcast_in_dim_reshape.3 = f32[3,1,2,512,512]{4,3,0,2,1:T(8,128)} reshape(f32[3,2,128,4,512]{4,3,2,0,1:T(4,128)} %maximum_bitcast_fusion) | data formatting | bytes 12582912 | tf_op jit(solution)/shard_map/broadcast_in_dim;reshape | solution.py:84
  189.7 5.2 %fusion.2 = f32[3,512,64]{1,2,0:S(1)} fusion(f32[3,512,64]{1,2,0:T(8,128)S(1)} %bitcast.207, f32[3,1,2,512,512]{4,3,0,2,1:T(8,128)} %broadcast_in_dim_reshape.3), kind=kOutput, calls=%fused_computation.10 | convolution fusion | flops 603979776 | bytes 3932160
  194.9 5.0 %fusion.3 = f32[3,512,64]{1,2,0:S(1)} fusion(f32[3,512,64]{1,2,0:T(8,128)S(1)} %bitcast.208, f32[3,1,2,512,512]{4,3,0,2,1:T(8,128)} %broadcast_in_dim_reshape.3), kind=kOutput, calls=%fused_computation.11 | convolution fusion | flops 603979776 | bytes 3932160
  199.9 3.2 fusion.4
  203.1 3.2 fusion.1
  206.3 0.1 add_bitcast_fusion.3
  206.4 0.9 pad_maximum_fusion
  207.4 0.3 all-gather.12.cloned.1.call-start
  208.2 0.6 gather_fusion
  208.9 1.1 fusion.17
  210.0 88.6 %all-gather.22.cloned.1.call-done = f32[48,2,2,512,32]{3,4,1,0,2:T(8,128)} async-done(((f32[3,2,2,512,32]{3,4,1,0,2:T(8,128)}), f32[48,2,2,512,32]{3,4,1,0,2:T(8,128)}) %all-gather.22.cloned.1.call-update) | async-done | bytes 12582928 | tf_op jit(solution)/shard_map/all_gather | solution.py:85
  298.5 12.0 %copy.73 = f32[16,3,2,2,512,32]{4,5,0,3,2,1:T(8,128)} copy(f32[16,3,2,2,512,32]{4,5,2,1,0,3:T(8,128)} %bitcast.204) | data formatting | bytes 25165824 | tf_op jit(solution)/shard_map/all_gather | solution.py:85
  310.6 10.6 %fusion.20 = (f32[1,2,2,512,16,32]{3,5,4,2,1,0:T(8,128)}, f32[1,2,2,512,16,32]{3,5,4,2,1,0:T(8,128)}, f32[1,2,2,512,16,32]{3,5,4,2,1,0:T(8,128)}) fusion(f32[3,2,2,512,16,32]{3,5,4,2,1,0:T(8,128)} %bitcast.191), kind=kLoop, calls=%fused_computation.61 | loop fusion | bytes 25165824 | tf_op jit(solution)/shard_map/slice | solution.py:61
  321.1 48.1 %all-gather.12.cloned.1.call-done = f32[1,3,2,512,512]{4,3,2,1,0:T(8,128)} async-done(((f32[1,3,2,64,512]{4,3,2,1,0:T(8,128)}), f32[1,3,2,512,512]{4,3,2,1,0:T(8,128)}) %all-gather.12.cloned.1.call-update) | async-done | bytes 6291472 | tf_op jit(solution)/shard_map/all_gather | solution.py:83
  369.2 5.6 %fusion.14 = f32[512,2,512]{2,0,1:T(8,128)S(1)} fusion(f32[1,2,2,512,512]{3,4,2,1,0:T(8,128)} %bitcast.200, f32[1,3,2,512,512]{4,3,2,1,0:T(8,128)} %all-gather.12.cloned.1.call-done), kind=kOutput, calls=%fused_computation.34 | convolution fusion | flops 3221225472 | bytes 5242880 | tf_op jit(solution)/shard_map/dot_general | solution.py:49
  374.9 5.0 %fusion.13 = f32[512,2,512]{2,0,1:T(8,128)S(1)} fusion(f32[1,2,2,512,512]{3,4,2,1,0:T(8,128)S(1)} %bitcast.201, f32[1,3,2,512,512]{4,3,2,1,0:T(8,128)} %all-gather.12.cloned.1.call-done), kind=kOutput, calls=%fused_computation.33 | convolution fusion | flops 3221225472 | bytes 5242880 | tf_op jit(solution)/shard_map/dot_general | solution.py:52
  379.9 5.3 %fusion.10 = f32[512,2,512]{2,0,1:T(8,128)S(1)} fusion(f32[1,2,2,512,512]{3,4,2,1,0:T(8,128)S(1)} %bitcast.196, f32[1,3,2,512,512]{4,3,2,1,0:T(8,128)} %all-gather.12.cloned.1.call-done), kind=kOutput, calls=%fused_computation.30 | convolution fusion | flops 3221225472 | bytes 5242880 | tf_op jit(solution)/shard_map/dot_general | solution.py:49
  385.2 3.6 fusion.9
  388.8 3.6 fusion.6
  392.4 3.8 fusion.5
  396.2 3.6 subtract_bitcast_fusion
  399.8 3.6 add_bitcast_fusion
  403.4 3.8 subtract_bitcast_fusion.1
  407.3 3.6 add_bitcast_fusion.1
  410.9 3.6 subtract_bitcast_fusion.2
  414.5 3.7 add_bitcast_fusion.2
  418.2 1.6 fusion
  419.8 2.5 copy.62
  (38 shorter events, 0.4 us)
Async XLA Ops:
  6.5 201.7 %copy-start = (f32[1,8,2,64,512]{4,3,2,1,0:T(8,128)S(1)}, f32[1,8,2,64,512]{4,3,2,1,0:T(8,128)}, u32[]{:S(2)}) copy-start(f32[1,8,2,64,512]{4,3,2,1,0:T(8,128)} %param.5) | copy-start | bytes 6291460
  6.5 137.2 %all-gather.14.cloned.1.call-start = ((), (), s32[]{:S(2)}) async-start(), calls=%async_computation.1 | async-start | bytes 2359296 | tf_op jit(solution)/shard_map/all_gather | solution.py:22
  43.3 108.7 %all-gather.16.cloned.1.call-start = ((), (), s32[]{:S(2)}) async-start(), calls=%async_computation.2 | async-start | bytes 2359296 | tf_op jit(solution)/shard_map/all_gather | solution.py:22
  78.7 81.1 %all-gather.18.cloned.1.call-start = ((), (), s32[]{:S(2)}) async-start(), calls=%async_computation.3 | async-start | bytes 1966080 | tf_op jit(solution)/shard_map/all_gather | solution.py:22
  107.8 65.1 %all-gather.20.cloned.1.call-start = ((), (), s32[]{:S(2)}) async-start(), calls=%async_computation.4 | async-start | bytes 1966080 | tf_op jit(solution)/shard_map/all_gather | solution.py:22
  139.8 158.7 %all-gather.22.cloned.1.call-start = ((), (), s32[]{:S(2)}) async-start(), calls=%async_computation.5 | async-start | bytes 13369344 | tf_op jit(solution)/shard_map/all_gather | solution.py:85
  139.8 2.2 copy-start.7
  189.7 10.2 %copy-start.2 = (f32[3,1,2,512,512]{4,3,0,2,1:T(8,128)S(1)}, f32[3,1,2,512,512]{4,3,0,2,1:T(8,128)}, u32[]{:S(2)}) copy-start(f32[3,1,2,512,512]{4,3,0,2,1:T(8,128)} %broadcast_in_dim_reshape.3) | copy-start | bytes 18874372
  206.3 2.6 copy-start.8
  207.4 161.9 %all-gather.12.cloned.1.call-start = ((), (), s32[]{:S(2)}) async-start(), calls=%async_computation | async-start | bytes 7077888 | tf_op jit(solution)/shard_map/all_gather | solution.py:83
  369.2 5.7 %copy-start.5 = (f32[1,2,2,512,16,32]{3,5,4,2,1,0:T(8,128)S(1)}, f32[1,2,2,512,16,32]{3,5,4,2,1,0:T(8,128)}, u32[]{:S(2)}) copy-start(f32[1,2,2,512,16,32]{3,5,4,2,1,0:T(8,128)} %get-tuple-element.5) | copy-start | bytes 12582916
  374.9 5.0 %copy-start.4 = (f32[1,2,2,512,16,32]{3,5,4,2,1,0:T(8,128)S(1)}, f32[1,2,2,512,16,32]{3,5,4,2,1,0:T(8,128)}, u32[]{:S(2)}) copy-start(f32[1,2,2,512,16,32]{3,5,4,2,1,0:T(8,128)} %get-tuple-element.6) | copy-start | bytes 12582916
  374.9 10.3 %copy-start.6 = (f32[1,3,2,512,512]{4,3,2,1,0:T(8,128)S(1)}, f32[1,3,2,512,512]{4,3,2,1,0:T(8,128)}, u32[]{:S(2)}) copy-start(f32[1,3,2,512,512]{4,3,2,1,0:T(8,128)} %all-gather.12.cloned.1.call-done) | copy-start | bytes 18874372
  385.2 3.6 copy-start.3
  418.2 4.1 copy-start.1
Sparse Core Ops, SparseCore 0:
  43.4 21.2 all-gather.13
  78.8 36.6 all-gather.15
  117.2 27.3 all-gather.17
  146.2 26.6 all-gather.19
  207.5 91.0 all-gather.21
  300.0 69.1 all-gather.11
